TPU v7x, 32 devices: a whole 2x2x4 slice. The times are simulated.
32 devices in a mesh: tm: 4 (over x, core), space: 8 (over z, y).
Axes of the slice: x: 2, y: 2, z: 4, core: 2. Of those that a mesh axis runs over, the one named last changes fastest.
Arguments:
- obs_perturb: bfloat16 [4, 32, 1024, 256], P('tm', 'space'), may hold values from -1.796875 to 1.796875
- innovation: float32 [4, 32, 1024], P('tm', 'space'), may hold values from -12 to 12
- error_weight: float32 [4, 32, 1024], P('tm', 'space'), may hold values from 0.5 to 2
- obs_column: int32 [4, 32, 1024], P('tm', 'space'), may hold values from 0 to 31
- obs_count: int32 [4, 32], P('tm', 'space'), may hold values from 64 to 1024, as said below
- radius: int32 [32], P('space'), may hold values from 56 to 80
- states: bfloat16 [8, 1024, 16, 256], P('tm', 'space'), may hold values from -6 to 6
Outputs:
- analysis: bfloat16 [8, 1024, 16, 256], P('tm', 'space')
Inputs may be any that keep to these rules, and one draw needn't show every extreme that they name: `obs_count`: at most 1024; some slot and region holds exactly 1024 in every draw.
All inputs are finite; a program needn't handle non-finite values.
Results may differ from a plain program's by a relative error of at most 0.0065.
Values may be sent and summed in bfloat16 or wider, within the bound.
A program may use at most 64 MiB of HBM per device.

v0:
```python
import jax
import jax.numpy as jnp
from jax import lax
from jax.sharding import PartitionSpec as P

HC = 32
NS_ITERS = 5


INFLATION = 1.1
HIGHEST = lax.Precision.HIGHEST


def with_halo(block, sides, width):
    for axis, dim in sides:
        count = lax.axis_size(axis)
        forward = [(i, i + 1) for i in range(count - 1)]
        forward.append((count - 1, 0))
        backward = [(target, source) for source, target in forward]
        low = lax.ppermute(
            lax.slice_in_dim(block, block.shape[dim] - width, None, axis=dim), axis, forward
        )
        high = lax.ppermute(lax.slice_in_dim(block, 0, width, axis=dim), axis, backward)
        block = jnp.concatenate([low, block, high], axis=dim)
    return block


def taper(column, radius, offset, width):
    distance = jnp.abs(column.astype(jnp.float32) + 0.5 - 0.5 * width - offset * width)
    ratio = jnp.minimum(distance / radius.astype(jnp.float32), 1.0)
    return jnp.square(1.0 - ratio * ratio)


def ensemble_transform(gram_sum, innov_sum):
    members = gram_sum.shape[-1]
    identity = jnp.eye(members, dtype=jnp.float32)
    system = gram_sum + (members - 1) / INFLATION * identity
    frobenius = jnp.sqrt(jnp.sum(system * system, axis=(1, 2)))
    root_now = system / frobenius[:, None, None]
    inverse = jnp.broadcast_to(identity, system.shape)
    for iteration in range(NS_ITERS):
        middle = 1.5 * identity - 0.5 * jnp.einsum(
            "nij,njk->nik", inverse, root_now, precision=HIGHEST
        )
        root_now = jnp.einsum("nij,njk->nik", root_now, middle, precision=HIGHEST)
        inverse = jnp.einsum("nij,njk->nik", middle, inverse, precision=HIGHEST)
    spread_part = jnp.sqrt(members - 1.0) * inverse / jnp.sqrt(frobenius)[:, None, None]
    half_step = jnp.einsum("nij,nj->ni", inverse, innov_sum, precision=HIGHEST)
    mean_part = jnp.einsum("nij,nj->ni", inverse, half_step, precision=HIGHEST) / frobenius[:, None]
    return spread_part + mean_part[:, :, None]


def spread_edges(margin, regions):
    filler = jnp.zeros((regions - 4,) + margin.shape[1:], margin.dtype)
    return jnp.concatenate([margin[:2], filler, margin[-2:]], axis=0)


def shards(obs_perturb, innovation, error_weight, obs_column, obs_count, radius, states):
    slot_count, regions, capacity, members = obs_perturb.shape
    position = lax.broadcasted_iota(jnp.int32, (slot_count, regions, capacity), 2)
    present = (position < obs_count[:, :, None]).astype(jnp.float32)
    base_weight = error_weight * present
    gram_local = jnp.zeros((regions + 4, members, members), jnp.float32)
    vec_local = jnp.zeros((regions + 4, members), jnp.float32)
    for offset in range(-2, 3):
        weight = base_weight * taper(obs_column, radius[None, :, None], offset, HC)
        weighted = (obs_perturb * weight[..., None]).astype(jnp.bfloat16)
        gram_part = jnp.einsum(
            "srok,srol->rkl", weighted, obs_perturb, preferred_element_type=jnp.float32
        )
        vec_part = jnp.einsum(
            "srok,sro->rk",
            weighted,
            innovation,
            precision=HIGHEST,
            preferred_element_type=jnp.float32,
        )
        gram_local = gram_local + jnp.pad(gram_part, ((offset + 2, 2 - offset), (0, 0), (0, 0)))
        vec_local = vec_local + jnp.pad(vec_part, ((offset + 2, 2 - offset), (0, 0)))
    edge_gram = jnp.concatenate([gram_local[:2], gram_local[regions + 2 :]], axis=0)
    edge_vec = jnp.concatenate([vec_local[:2], vec_local[regions + 2 :]], axis=0)
    inner_gram = gram_local[2 : regions + 2]
    inner_vec = vec_local[2 : regions + 2]
    margin_gram, margin_vec = (
        with_halo(edge_gram.astype(jnp.bfloat16), (("space", 0),), 2).astype(edge_gram.dtype),
        with_halo(edge_vec.astype(jnp.bfloat16), (("space", 0),), 2).astype(edge_vec.dtype),
    )
    inner_gram = inner_gram + spread_edges(margin_gram, regions)
    inner_vec = inner_vec + spread_edges(margin_vec, regions)
    mine_gram, mine_vec = (
        lax.psum_scatter(inner_gram, "tm", scatter_dimension=0, tiled=True),
        lax.psum_scatter(inner_vec, "tm", scatter_dimension=0, tiled=True),
    )
    local_transform = ensemble_transform(mine_gram, mine_vec).astype(jnp.bfloat16)
    transform = lax.all_gather(local_transform, "tm", axis=0, tiled=True)
    bordered = with_halo(transform, (("space", 0),), 1)
    lag_count = states.shape[0]
    levels = states.shape[2]
    mean_state = jnp.mean(states.astype(jnp.float32), axis=-1, keepdims=True)
    anomaly = (
        (states - mean_state).astype(jnp.bfloat16).reshape(lag_count, regions, HC, levels, members)
    )
    half_width = HC // 2
    centre = jnp.einsum(
        "lrcvk,rkj->lrcvj", anomaly, bordered[1 : regions + 1], preferred_element_type=jnp.float32
    )
    western = jnp.einsum(
        "lrcvk,rkj->lrcvj",
        anomaly[:, :, :half_width],
        bordered[:regions],
        preferred_element_type=jnp.float32,
    )
    eastern = jnp.einsum(
        "lrcvk,rkj->lrcvj",
        anomaly[:, :, half_width:],
        bordered[2 : regions + 2],
        preferred_element_type=jnp.float32,
    )
    beside = jnp.concatenate([western, eastern], axis=2)
    blend_weight = jnp.abs((jnp.arange(HC, dtype=jnp.float32) + 0.5) / HC - 0.5).reshape(
        1, 1, HC, 1, 1
    )
    result = (
        mean_state.reshape(lag_count, regions, HC, levels, 1)
        + (1.0 - blend_weight) * centre
        + blend_weight * beside
    )
    return result.reshape(states.shape).astype(jnp.bfloat16)


def solution(mesh):
    return jax.shard_map(
        shards,
        mesh=mesh,
        in_specs=(
            P("tm", "space", None, None),
            P("tm", "space", None),
            P("tm", "space", None),
            P("tm", "space", None),
            P("tm", "space"),
            P("space"),
            P("tm", "space", None, None),
        ),
        out_specs=P("tm", "space", None, None),
        check_vma=False,
    )
```

profile of v0, /device:TPU:1, one launch (start us, length us, event | category | flops | bytes accessed | tf_op | source)
XLA Modules:
  0.0 100.9 jit_solution(17590336519601874574)
XLA Ops:
  6.5 0.7 convert_element_type.89
  7.2 0.8 multiply_bitcast_fusion.4
  8.1 3.8 %fusion.13 = f32[4,256,256]{2,1,0:T(8,128)S(1)} fusion(bf16[1,4,1024,256]{3,2,1,0:T(8,128)(2,1)} %param.7, f32[4,1024]{1,0:T(4,128)S(1)} %get-tuple-element.19), kind=kOutput, calls=%fused_computation.22 | convolution fusion | flops 540016640 | bytes 3162112 | tf_op jit(solution)/shard_map/srok,srol->rkl/dot_general | solution.py:68
  11.9 1.8 %fusion.15 = f32[4,256,256]{2,1,0:T(8,128)S(1)} fusion(bf16[1,4,1024,256]{3,2,1,0:T(8,128)(2,1)S(1)} %copy-done.4, f32[4,1024]{1,0:T(4,128)S(1)} %get-tuple-element.18), kind=kOutput, calls=%fused_computation.24 | convolution fusion | flops 540016640 | bytes 3162112 | tf_op jit(solution)/shard_map/srok,srol->rkl/dot_general | solution.py:68
  13.7 1.8 %fusion.17 = f32[4,256,256]{2,1,0:T(8,128)S(1)} fusion(bf16[1,4,1024,256]{3,2,1,0:T(8,128)(2,1)S(1)} %copy-done.4, f32[4,1024]{1,0:T(4,128)S(1)} %get-tuple-element.17), kind=kOutput, calls=%fused_computation.26 | convolution fusion | flops 540016640 | bytes 3162112 | tf_op jit(solution)/shard_map/srok,srol->rkl/dot_general | solution.py:68
  15.5 1.8 %fusion.19 = f32[4,256,256]{2,1,0:T(8,128)S(1)} fusion(bf16[1,4,1024,256]{3,2,1,0:T(8,128)(2,1)S(1)} %copy-done.4, f32[4,1024]{1,0:T(4,128)S(1)} %get-tuple-element.16), kind=kOutput, calls=%fused_computation.28 | convolution fusion | flops 540016640 | bytes 3162112 | tf_op jit(solution)/shard_map/srok,srol->rkl/dot_general | solution.py:68
  17.3 1.8 %fusion.21 = f32[4,256,256]{2,1,0:T(8,128)S(1)} fusion(bf16[1,4,1024,256]{3,2,1,0:T(8,128)(2,1)S(1)} %copy-done.4, f32[4,1024]{1,0:T(4,128)S(1)} %get-tuple-element.15), kind=kOutput, calls=%fused_computation.30 | convolution fusion | flops 540016640 | bytes 3162112 | tf_op jit(solution)/shard_map/srok,srol->rkl/dot_general | solution.py:68
  19.6 2.1 %collective-permute-start = (bf16[2,256,256]{2,1,0:T(8,128)(2,1)S(1)}, bf16[2,256,256]{2,1,0:T(8,128)(2,1)S(1)}, u32[]{:S(2)}, u32[]{:S(2)}) collective-permute-start(bf16[2,256,256]{2,1,0:T(8,128)(2,1)S(1)} %get-tuple-element.11), channel_id=1, source_target_pairs={{0,1},{1,2},{2,3},{3,4},{4,5},{5,6},{6,7},{7,0},{8,9},{9,10},{10,1... | collective-permute-start | bytes 786440 | tf_op jit(solution)/shard_map/ppermute | solution.py:20
  21.7 3.1 %collective-permute-start.1 = (bf16[2,256,256]{2,1,0:T(8,128)(2,1)S(1)}, bf16[2,256,256]{2,1,0:T(8,128)(2,1)S(1)}, u32[]{:S(2)}, u32[]{:S(2)}) collective-permute-start(bf16[2,256,256]{2,1,0:T(8,128)(2,1)S(1)} %get-tuple-element.12), channel_id=1, source_target_pairs={{1,0},{2,1},{3,2},{4,3},{5,4},{6,5},{7,6},{0,7},{9,8},{10,9},{11,1... | collective-permute-start | bytes 786440 | tf_op jit(solution)/shard_map/ppermute | solution.py:23
  24.8 1.4 %fusion.35 = f32[4,1,256]{2,1,0:T(1,128)S(1)} fusion(bf16[1,4,1024,256]{3,2,1,0:T(8,128)(2,1)S(1)} %copy-done.4, f32[4,1024]{1,0:T(4,128)S(1)} %get-tuple-element.15, f32[4,1024,1]{1,0,2:T(4,128)S(1)} %bitcast.127), kind=kOutput, calls=%fused_computation.37 | convolution fusion | flops 15728640 | bytes 2134016 | tf_op jit(solution)/shard_map/srok,sro->rk/dot_general | solution.py:71
  26.2 1.5 %fusion.32 = f32[4,1,256]{2,1,0:T(1,128)S(1)} fusion(bf16[1,4,1024,256]{3,2,1,0:T(8,128)(2,1)S(1)} %copy-done.4, f32[4,1024]{1,0:T(4,128)S(1)} %get-tuple-element.16, f32[4,1024,1]{1,0,2:T(4,128)S(1)} %bitcast.131), kind=kOutput, calls=%fused_computation.36 | convolution fusion | flops 15728640 | bytes 2134016 | tf_op jit(solution)/shard_map/srok,sro->rk/dot_general | solution.py:71
  27.7 1.5 %fusion.29 = f32[4,1,256]{2,1,0:T(1,128)S(1)} fusion(bf16[1,4,1024,256]{3,2,1,0:T(8,128)(2,1)S(1)} %copy-done.4, f32[4,1024]{1,0:T(4,128)S(1)} %get-tuple-element.17, f32[4,1024,1]{1,0,2:T(4,128)S(1)} %bitcast.130), kind=kOutput, calls=%fused_computation.35 | convolution fusion | flops 15728640 | bytes 2134016 | tf_op jit(solution)/shard_map/srok,sro->rk/dot_general | solution.py:71
  29.2 3.2 %collective-permute-done = bf16[2,256,256]{2,1,0:T(8,128)(2,1)S(1)} collective-permute-done((bf16[2,256,256]{2,1,0:T(8,128)(2,1)S(1)}, bf16[2,256,256]{2,1,0:T(8,128)(2,1)S(1)}, u32[]{:S(2)}, u32[]{:S(2)}) %collective-permute-start) | collective-permute-done | bytes 262176 | tf_op jit(solution)/shard_map/ppermute | solution.py:20
  32.3 1.9 %collective-permute-done.1 = bf16[2,256,256]{2,1,0:T(8,128)(2,1)S(1)} collective-permute-done((bf16[2,256,256]{2,1,0:T(8,128)(2,1)S(1)}, bf16[2,256,256]{2,1,0:T(8,128)(2,1)S(1)}, u32[]{:S(2)}, u32[]{:S(2)}) %collective-permute-start.1) | collective-permute-done | bytes 262176 | tf_op jit(solution)/shard_map/ppermute | solution.py:23
  34.3 1.1 %slice_add_fusion = f32[4,256,256]{2,1,0:T(8,128)} fusion(f32[8,256,256]{2,1,0:T(8,128)S(1)} %get-tuple-element.8, f32[2,256,256]{2,1,0:T(8,128)S(1)} %get-tuple-element.10, f32[2,256,256]{2,1,0:T(8,128)S(1)} %get-tuple-element.9), kind=kLoop, calls=%fused_computation.53 | loop fusion | flops 524288 | bytes 3145728 | tf_op jit(solution)/shard_map/add | solution.py:88
  35.5 2.7 %fusion.26 = f32[4,1,256]{2,1,0:T(1,128)S(1)} fusion(bf16[1,4,1024,256]{3,2,1,0:T(8,128)(2,1)} %param.7, f32[4,1024]{1,0:T(4,128)S(1)} %get-tuple-element.18, f32[4,1024,1]{1,0,2:T(4,128)S(1)} %bitcast.129), kind=kOutput, calls=%fused_computation.34 | convolution fusion | flops 15728640 | bytes 2134016 | tf_op jit(solution)/shard_map/srok,sro->rk/dot_general | solution.py:71
  38.2 2.8 %fusion.23 = f32[4,1,256]{2,1,0:T(1,128)S(1)} fusion(bf16[1,4,1024,256]{3,2,1,0:T(8,128)(2,1)} %param.7, f32[4,1024]{1,0:T(4,128)S(1)} %get-tuple-element.19, f32[4,1024,1]{1,0,2:T(4,128)S(1)} %bitcast.128), kind=kOutput, calls=%fused_computation.33 | convolution fusion | flops 15728640 | bytes 2134016 | tf_op jit(solution)/shard_map/srok,sro->rk/dot_general | solution.py:71
  41.4 3.9 %collective-permute-start.3 = (bf16[2,256]{1,0:T(2,128)(2,1)S(1)}, bf16[2,256]{1,0:T(2,128)(2,1)S(1)}, u32[]{:S(2)}, u32[]{:S(2)}) collective-permute-start(bf16[2,256]{1,0:T(2,128)(2,1)S(1)} %get-tuple-element.23), channel_id=1, source_target_pairs={{1,0},{2,1},{3,2},{4,3},{5,4},{6,5},{7,6},{0,7},{9,8},{10,9},{11,1... | collective-permute-start | bytes 3080 | tf_op jit(solution)/shard_map/ppermute | solution.py:23
  45.9 0.6 dynamic-slice
  46.6 7.7 %all-reduce.10 = f32[4,256]{1,0:T(4,128)S(1)} all-reduce(f32[4,256]{1,0:T(4,128)S(1)} %slice_add_fusion.1), channel_id=4, replica_groups=mesh['tm'=4,'space'=8] {'tm'}, use_global_device_ids=true, to_apply=%region_3.4.clone | all-reduce | flops 1024 | bytes 8192
  54.2 7.1 %reduce-scatter.2.cloned.1.call-done = f32[1,256,256]{2,1,0:T(8,128)} async-done(((f32[4,256,256]{2,1,0:T(8,128)}), f32[1,256,256]{2,1,0:T(8,128)}) %reduce-scatter.2.cloned.1.call-update) | async-done | bytes 262160 | tf_op jit(solution)/shard_map/reduce_scatter | solution.py:91
  61.4 1.7 %multiply_reduce_fusion = f32[]{:T(128)} fusion(f32[1,256,256]{2,1,0:T(8,128)} %reduce-scatter.2.cloned.1.call-done), kind=kLoop, calls=%fused_computation.69 | loop fusion | flops 327679 | bytes 262148 | tf_op jit(solution)/shard_map/reduce_sum | solution.py:38
  63.8 1.3 %fusion.42 = f32[256,256]{1,0:T(8,128)S(1)} fusion(f32[1,256,256]{2,1,0:T(8,128)} %reduce-scatter.2.cloned.1.call-done, f32[]{:T(128)S(6)} %sqrt.8), kind=kOutput, calls=%fused_computation.49 | convolution fusion | flops 201916416 | bytes 524292 | tf_op jit(solution)/shard_map/nij,njk->nik/dot_general | solution.py:42
  70.0 0.9 convolution_bitcast_fusion.2
  71.4 7.3 %all-gather = bf16[1024,256]{1,0:T(8,128)(2,1)S(1)} all-gather(bf16[256,256]{1,0:T(8,128)(2,1)S(1)} %add_convert_fusion), channel_id=2, replica_groups=mesh['tm'=4,'space'=8] {'tm'}, dimensions={0}, use_global_device_ids=true | all-gather | bytes 655360 | tf_op jit(solution)/shard_map/all_gather | solution.py:95
  78.7 1.3 %collective-permute-start.4 = (bf16[1,256,256]{2,1,0:T(8,128)(2,1)S(1)}, bf16[1,256,256]{2,1,0:T(8,128)(2,1)S(1)}, u32[]{:S(2)}, u32[]{:S(2)}) collective-permute-start(bf16[1,256,256]{2,1,0:T(8,128)(2,1)S(1)} %get-tuple-element.13), channel_id=1, source_target_pairs={{0,1},{1,2},{2,3},{3,4},{4,5},{5,6},{6,7},{7,0},{8,9},{9,10},{10,1... | collective-permute-start | bytes 393224 | tf_op jit(solution)/shard_map/ppermute | solution.py:20
  80.0 1.7 %fusion = bf16[2,128,16,256]{3,2,1,0:T(8,128)(2,1)} fusion(bf16[2,128,16,256]{3,2,1,0:T(8,128)(2,1)S(1)} %copy-done.1, f32[2,128,16]{2,1,0:T(8,128)S(1)} %broadcast_multiply_fusion), kind=kLoop, calls=%fused_computation.7 | loop fusion | flops 3145728 | bytes 4210688 | tf_op jit(solution)/shard_map/convert_element_type | solution.py:101
  81.7 2.4 %copy.36 = bf16[2,4,32,16,256]{4,2,3,0,1:T(8,128)(2,1)S(1)} copy(bf16[2,4,32,16,256]{4,3,2,1,0:T(8,128)(2,1)} %bitcast.132) | data formatting | bytes 4194304 | tf_op jit(solution)/shard_map/reshape | solution.py:101
  84.2 3.0 %collective-permute-start.5 = (bf16[1,256,256]{2,1,0:T(8,128)(2,1)S(1)}, bf16[1,256,256]{2,1,0:T(8,128)(2,1)S(1)}, u32[]{:S(2)}, u32[]{:S(2)}) collective-permute-start(bf16[1,256,256]{2,1,0:T(8,128)(2,1)S(1)} %get-tuple-element.14), channel_id=1, source_target_pairs={{1,0},{2,1},{3,2},{4,3},{5,4},{6,5},{7,6},{0,7},{9,8},{10,9},{11,1... | collective-permute-start | bytes 393224 | tf_op jit(solution)/shard_map/ppermute | solution.py:23
  87.6 1.9 %collective-permute-done.5 = bf16[1,256,256]{2,1,0:T(8,128)(2,1)S(1)} collective-permute-done((bf16[1,256,256]{2,1,0:T(8,128)(2,1)S(1)}, bf16[1,256,256]{2,1,0:T(8,128)(2,1)S(1)}, u32[]{:S(2)}, u32[]{:S(2)}) %collective-permute-start.5) | collective-permute-done | bytes 131104 | tf_op jit(solution)/shard_map/ppermute | solution.py:23
  90.0 1.4 %fusion.7 = bf16[2,4,32,16,256]{4,2,3,0,1:T(8,128)(2,1)S(1)} fusion(f32[2,4,16,16,256]{4,2,3,0,1:T(8,128)S(1)} %convolution_bitcast_fusion, f32[2,4,16,16,256]{4,2,3,0,1:T(8,128)S(1)} %convolution_bitcast_fusion.1, bf16[4,256,256,1,1]{2,1,4,3,0:T(8,128)(2,1)S(1)} %bitcast.136, f32[32]{0:T(128)S(1)} %get-tuple-element.28, f32[32]{0:T(128)S(1)} %get-tuple-element.29, ...), kind=kOutput, calls=%fused_computation.15 | convolution fusion | flops 543162368 | bytes 8929536 | tf_op jit(solution)/shard_map/lrcvk,rkj->lrcvj/dot_general | solution.py:104
  91.4 2.6 %copy.39 = bf16[2,4,32,16,256]{4,3,2,1,0:T(8,128)(2,1)} copy(bf16[2,4,32,16,256]{4,2,3,0,1:T(8,128)(2,1)S(1)} %fusion.7) | data formatting | bytes 4194304 | tf_op jit(solution)/shard_map/convert_element_type | solution.py:128
  (51 shorter events, 7.9 us)
Async XLA Ops:
  6.5 18.3 %copy-start = (f32[1,4,1024]{2,1,0:T(4,128)S(1)}, f32[1,4,1024]{2,1,0:T(4,128)}, u32[]{:S(2)}) copy-start(f32[1,4,1024]{2,1,0:T(4,128)} %param.8) | copy-start | bytes 49156
  6.5 54.8 %reduce-scatter.2.cloned.1.call-start = ((), (), s32[]{:S(2)}) async-start(), calls=%async_computation.1 | async-start | bytes 1310720 | tf_op jit(solution)/shard_map/reduce_scatter | solution.py:91
  8.1 3.8 %copy-start.4 = (bf16[1,4,1024,256]{3,2,1,0:T(8,128)(2,1)S(1)}, bf16[1,4,1024,256]{3,2,1,0:T(8,128)(2,1)}, u32[]{:S(2)}) copy-start(bf16[1,4,1024,256]{3,2,1,0:T(8,128)(2,1)} %param.7) | copy-start | bytes 6291460
  19.6 12.7 %collective-permute-start = (bf16[2,256,256]{2,1,0:T(8,128)(2,1)S(1)}, bf16[2,256,256]{2,1,0:T(8,128)(2,1)S(1)}, u32[]{:S(2)}, u32[]{:S(2)}) collective-permute-start(bf16[2,256,256]{2,1,0:T(8,128)(2,1)S(1)} %get-tuple-element.11), channel_id=1, source_target_pairs={{0,1},{1,2},{2,3},{3,4},{4,5},{5,6},{6,7},{7,0},{8,9},{9,10},{10,1... | collective-permute-start | bytes 786440 | tf_op jit(solution)/shard_map/ppermute | solution.py:20
  21.7 12.5 %collective-permute-start.1 = (bf16[2,256,256]{2,1,0:T(8,128)(2,1)S(1)}, bf16[2,256,256]{2,1,0:T(8,128)(2,1)S(1)}, u32[]{:S(2)}, u32[]{:S(2)}) collective-permute-start(bf16[2,256,256]{2,1,0:T(8,128)(2,1)S(1)} %get-tuple-element.12), channel_id=1, source_target_pairs={{1,0},{2,1},{3,2},{4,3},{5,4},{6,5},{7,6},{0,7},{9,8},{10,9},{11,1... | collective-permute-start | bytes 786440 | tf_op jit(solution)/shard_map/ppermute | solution.py:23
  38.1 7.1 %copy-start.1 = (bf16[2,128,16,256]{3,2,1,0:T(8,128)(2,1)S(1)}, bf16[2,128,16,256]{3,2,1,0:T(8,128)(2,1)}, u32[]{:S(2)}) copy-start(bf16[2,128,16,256]{3,2,1,0:T(8,128)(2,1)} %param.13) | copy-start | bytes 6291460
  38.2 7.8 %copy-start.5 = (u32[32]{0:T(128)S(1)}, u32[32]{0:T(128)}, u32[]{:S(2)}) copy-start(u32[32]{0:T(128)} %constant.77) | copy-start | bytes 388
  41.1 5.5 %collective-permute-start.2 = (bf16[2,256]{1,0:T(2,128)(2,1)S(1)}, bf16[2,256]{1,0:T(2,128)(2,1)S(1)}, u32[]{:S(2)}, u32[]{:S(2)}) collective-permute-start(bf16[2,256]{1,0:T(2,128)(2,1)S(1)} %get-tuple-element.22), channel_id=1, source_target_pairs={{0,1},{1,2},{2,3},{3,4},{4,5},{5,6},{6,7},{7,0},{8,9},{9,10},{10,1... | collective-permute-start | bytes 3080 | tf_op jit(solution)/shard_map/ppermute | solution.py:20
  41.4 5.2 %collective-permute-start.3 = (bf16[2,256]{1,0:T(2,128)(2,1)S(1)}, bf16[2,256]{1,0:T(2,128)(2,1)S(1)}, u32[]{:S(2)}, u32[]{:S(2)}) collective-permute-start(bf16[2,256]{1,0:T(2,128)(2,1)S(1)} %get-tuple-element.23), channel_id=1, source_target_pairs={{1,0},{2,1},{3,2},{4,3},{5,4},{6,5},{7,6},{0,7},{9,8},{10,9},{11,1... | collective-permute-start | bytes 3080 | tf_op jit(solution)/shard_map/ppermute | solution.py:23
  61.4 4.0 %copy-start.3 = (f32[1,256,256]{2,1,0:T(8,128)S(1)}, f32[1,256,256]{2,1,0:T(8,128)}, u32[]{:S(2)}) copy-start(f32[1,256,256]{2,1,0:T(8,128)} %reduce-scatter.2.cloned.1.call-done) | copy-start | bytes 786436
  78.7 8.4 %collective-permute-start.4 = (bf16[1,256,256]{2,1,0:T(8,128)(2,1)S(1)}, bf16[1,256,256]{2,1,0:T(8,128)(2,1)S(1)}, u32[]{:S(2)}, u32[]{:S(2)}) collective-permute-start(bf16[1,256,256]{2,1,0:T(8,128)(2,1)S(1)} %get-tuple-element.13), channel_id=1, source_target_pairs={{0,1},{1,2},{2,3},{3,4},{4,5},{5,6},{6,7},{7,0},{8,9},{9,10},{10,1... | collective-permute-start | bytes 393224 | tf_op jit(solution)/shard_map/ppermute | solution.py:20
  84.2 5.4 %collective-permute-start.5 = (bf16[1,256,256]{2,1,0:T(8,128)(2,1)S(1)}, bf16[1,256,256]{2,1,0:T(8,128)(2,1)S(1)}, u32[]{:S(2)}, u32[]{:S(2)}) collective-permute-start(bf16[1,256,256]{2,1,0:T(8,128)(2,1)S(1)} %get-tuple-element.14), channel_id=1, source_target_pairs={{1,0},{2,1},{3,2},{4,3},{5,4},{6,5},{7,6},{0,7},{9,8},{10,9},{11,1... | collective-permute-start | bytes 393224 | tf_op jit(solution)/shard_map/ppermute | solution.py:23
  87.6 2.4 %copy-start.2 = (bf16[2,128,16,256]{3,2,1,0:T(8,128)(2,1)S(1)}, bf16[2,128,16,256]{3,2,1,0:T(8,128)(2,1)}, u32[]{:S(2)}) copy-start(bf16[2,128,16,256]{3,2,1,0:T(8,128)(2,1)} %fusion) | copy-start | bytes 6291460
Sparse Core Ops, SparseCore 0:
  35.6 25.7 reduce-scatter.1
where the time goes:
time: 103 us; the launch traced here: 101 us
  matrix products  30.5 us (30%)
  blocking collectives  14.9 us (14%)
  between operations  14.5 us (14%)
  waiting for transfers between devices  14.2 us (14%)
  starting transfers between devices  13.7 us (13%)
  other arithmetic  7.28 us (7%)
  local copies, waits for them, and re-layouts  5.8 us (6%)
    dot_general x5, matrix products, shards(): jnp.einsum('srok,srol->rkl', weighted, obs_perturb, preferred_element_typ...  11 us
    ppermute x3, starting transfers between devices, with_halo(): lax.ppermute(lax.slice_in_dim(block, 0, width, axis=dim), axis, backward)  10 us
    dot_general x5, matrix products, shards(): jnp.einsum('srok,sro->rk', weighted, innovation, precision=HIGHEST, prefe...  9.87 us
    unnamed x1, blocking collectives  7.67 us
    all_gather x1, blocking collectives, shards(): transform = lax.all_gather(local_transform, 'tm', axis=0, tiled=True)  7.28 us
    reduce_scatter x1, waiting for transfers between devices, shards(): lax.psum_scatter(inner_gram, 'tm', scatter_dimension=0, tiled=True)  7.12 us
    ppermute x3, waiting for transfers between devices, with_halo(): lax.ppermute(lax.slice_in_dim(block, 0, width, axis=dim), axis, backward)  3.87 us
    ppermute x3, starting transfers between devices, with_halo(): lax.ppermute(lax.slice_in_dim(block, block.shape[dim] - width, None, axis...  3.7 us
  transfers between devices with their start and end apart: 7, of which 4 were waited for; matrix products, arithmetic and copies ran while one was open for 16% of the time, Pallas kernels for 0%

commit v1 on v0

v1 whole, which is shorter than its diff:
```python
import functools

import jax
import jax.numpy as jnp
from jax import lax
from jax.experimental import pallas as pl
from jax.experimental.pallas import tpu as pltpu
from jax.sharding import PartitionSpec as P

HC = 32
NS_ITERS = 5
INFLATION = 1.1
HALO = 2
REACH = 2 * HALO + 1
EXTRA = 16
MESH = pl.DeviceIdType.MESH
F32 = jnp.float32
BF16 = jnp.bfloat16


def iota2(shape, dim):
    return lax.broadcasted_iota(jnp.int32, shape, dim)


def pack(matrix, row):
    half = matrix.shape[0] // 2
    a, b, c = matrix[:half, :half], matrix[:half, half:], matrix[half:, half:]
    i, j = iota2((half, half), 0), iota2((half, half), 1)
    top = jnp.concatenate([b, jnp.where(j >= i, a, c)], axis=1)
    diagonal = jnp.sum(jnp.where(i == j, c, 0.0), axis=0, keepdims=True)
    second = jnp.concatenate([diagonal, jnp.zeros_like(diagonal)], axis=1)
    place = iota2((EXTRA, 2 * half), 0)
    extra = jnp.where(place == 0, row, jnp.where(place == 1, second, 0.0))
    return top, extra


def unpack(block):
    half = block.shape[0] - EXTRA
    b, d = block[:half, :half], block[:half, half:]
    row = block[half : half + 1]
    diagonal = block[half + 1 : half + 2, :half]
    i, j = iota2((half, half), 0), iota2((half, half), 1)
    flipped = d.T
    a = jnp.where(j >= i, d, flipped)
    c = jnp.where(i > j, d, jnp.where(i < j, flipped, diagonal))
    matrix = jnp.concatenate(
        [jnp.concatenate([a, b], axis=1), jnp.concatenate([b.T, c], axis=1)], axis=0
    )
    return matrix, row


def split(x):
    high = x.astype(BF16)
    return high, (x - high.astype(F32)).astype(BF16)


def dot3(x, m_high, m_low):
    x_high, x_low = split(x)
    dot = functools.partial(jnp.dot, preferred_element_type=F32)
    return dot(x_high, m_high) + (dot(x_high, m_low) + dot(x_low, m_high))


def transform_parts(gram, vec):
    members = gram.shape[0]
    identity = (iota2(gram.shape, 0) == iota2(gram.shape, 1)).astype(F32)
    system = gram + (members - 1) / INFLATION * identity
    frob = jnp.sqrt(jnp.sum(jnp.sum(system * system, axis=0, keepdims=True), axis=1, keepdims=True))
    product = system * (1.0 / frob)
    inverse = None
    for step in range(NS_ITERS):
        middle = 1.5 * identity - 0.5 * product
        m = split(middle)
        last = step == NS_ITERS - 1
        if inverse is None:
            inverse = middle
            moved = dot3(product, *m)
        elif last:
            inverse = dot3(inverse, *m)
        else:
            both = dot3(jnp.concatenate([product, inverse], axis=0), *m)
            moved, inverse = both[:members], both[members:]
        if not last:
            product = dot3(moved, *m)
    m = split(inverse)
    rows = jnp.broadcast_to(vec, (8, members))
    wbar = dot3(dot3(rows, *m), *m)[0:1] / frob
    spread = inverse * (jnp.sqrt(F32(members - 1.0)) / jnp.sqrt(frob))
    return spread, wbar


def assimilate(
    n_tm, n_space,
    count_ref, radius_ref, obs_hbm, innov_ref, weight_ref, column_ref, out_ref,
    obs_v, obs_t, mine, recv, halo_out, halo_in, t_out, t_in,
    load_sem, rs_send, rs_recv, halo_send, halo_recv, t_send, b_send, t_recv,
):
    tm, sp = lax.axis_index("tm"), lax.axis_index("space")
    after, before = lax.rem(sp + 1, n_space), lax.rem(sp + n_space - 1, n_space)
    regions, capacity, members = obs_v.shape
    half = members // 2
    targets = regions + 2 * HALO

    loads = [
        pltpu.make_async_copy(obs_hbm.at[0, r], obs_v.at[r], load_sem.at[r]) for r in range(regions)
    ]
    for load in loads:
        load.start()

    barrier = pltpu.get_barrier_semaphore()
    peers = [lax.rem(tm + d, n_tm) for d in range(1, n_tm)]
    greeted = [(p, sp) for p in peers]
    greeted += [(t, s) for s in (before, after) for t in range(n_tm)]
    for t, s in greeted:
        pl.semaphore_signal(barrier, inc=1, device_id={"tm": t, "space": s}, device_id_type=MESH)

    shape = (regions, capacity)
    which = iota2(shape, 0)
    count = jnp.zeros(shape, jnp.int32)
    radius = jnp.zeros(shape, jnp.int32)
    for r in range(regions):
        count = jnp.where(which == r, count_ref[0, r], count)
        radius = jnp.where(which == r, radius_ref[r], radius)
    present = (iota2(shape, 1) < count).astype(F32)
    base = weight_ref[0] * present
    inverse_radius = 1.0 / radius.astype(F32)
    position = column_ref[0].astype(F32) + 0.5 - 0.5 * HC
    weights, pulls = [], []
    for offset in range(-HALO, HALO + 1):
        ratio = jnp.minimum(jnp.abs(position - offset * HC) * inverse_radius, 1.0)
        weight = base * jnp.square(1.0 - ratio * ratio)
        weights.append(weight)
        pulls.append(weight * innov_ref[0])

    first_row = iota2((EXTRA, capacity), 0) == 0

    def gram_of(target):
        total = None
        for r in range(max(0, target - 2 * HALO), min(regions, target + 1)):
            k = target - r
            weight = jnp.broadcast_to(weights[k][r : r + 1], (16, capacity)).astype(BF16)
            pull = jnp.where(first_row, pulls[k][r : r + 1], 0.0).astype(BF16)
            scaled = obs_t[r].reshape(members // 16, 16, capacity) * weight[None]
            left = jnp.concatenate([scaled.reshape(members, capacity), pull], axis=0)
            part = jnp.dot(left, obs_v[r], preferred_element_type=F32)
            total = part if total is None else total + part
        top, extra = pack(total[:members], total[members : members + 1])
        mine[target, :half] = top.astype(BF16)
        mine[target, half:] = extra.astype(BF16)

    def exchange(kind, block_of):
        copies = []
        for d, peer in enumerate(peers):
            copies.append(
                pltpu.make_async_remote_copy(
                    src_ref=mine.at[block_of(peer)],
                    dst_ref=recv.at[kind, tm],
                    send_sem=rs_send.at[kind, d],
                    recv_sem=rs_recv.at[kind, tm],
                    device_id={"tm": peer, "space": sp},
                    device_id_type=MESH,
                )
            )
        return copies

    def collect(kind, block):
        total = mine[block].astype(F32)
        for peer in peers:
            pltpu.make_async_copy(
                recv.at[kind, peer], recv.at[kind, peer], rs_recv.at[kind, peer]
            ).wait()
            total = total + recv[kind, peer].astype(F32)
        return total

    for r in range(regions):
        loads[r].wait()
        obs_t[r] = obs_v[r].T
    pl_wait = len(greeted)
    edges = [*range(HALO), *range(targets - HALO, targets)]
    for target in edges:
        gram_of(target)
    pl.semaphore_wait(barrier, pl_wait)
    edge_block = lambda p: lax.rem(p + regions + HALO, targets)
    inner_block = lambda p: p + HALO
    edge_copies = exchange(0, edge_block)
    for copy in edge_copies:
        copy.start()
    inner = list(range(HALO, targets - HALO))
    for target in inner:
        gram_of(target)
    inner_copies = exchange(1, inner_block)
    for copy in inner_copies:
        copy.start()

    halo_out[...] = collect(0, edge_block(tm)).astype(BF16)
    halo_copy = pltpu.make_async_remote_copy(
        src_ref=halo_out,
        dst_ref=halo_in,
        send_sem=halo_send,
        recv_sem=halo_recv,
        device_id={"tm": tm, "space": jnp.where(tm < HALO, after, before)},
        device_id_type=MESH,
    )
    halo_copy.start()
    total = collect(1, inner_block(tm))
    halo_copy.wait()
    gram, vec = unpack(total + halo_in[...].astype(F32))
    spread, wbar = transform_parts(gram, vec)
    top, extra = pack(spread, wbar)
    t_out[:half] = top.astype(BF16)
    t_out[half:] = extra.astype(BF16)

    def send_transform(t, s, slot, sem):
        return pltpu.make_async_remote_copy(
            src_ref=t_out,
            dst_ref=t_in.at[slot],
            send_sem=sem,
            recv_sem=t_recv.at[slot],
            device_id={"tm": t, "space": s},
            device_id_type=MESH,
        )

    low = [send_transform(t, before, regions + 1, b_send.at[t]) for t in range(n_tm)]
    high = [send_transform(t, after, 0, b_send.at[t]) for t in range(n_tm)]

    @pl.when(tm == 0)
    def _():
        for copy in low:
            copy.start()

    @pl.when(tm == n_tm - 1)
    def _():
        for copy in high:
            copy.start()

    t_copies = [send_transform(p, sp, tm + 1, t_send.at[d]) for d, p in enumerate(peers)]
    for copy in t_copies:
        copy.start()

    def place(slot, block):
        matrix, row = unpack(block.astype(F32))
        out_ref[slot] = (matrix + row).astype(BF16)

    place(tm + 1, t_out[...])
    for slot in [lax.rem(tm + d, n_tm) + 1 for d in range(1, n_tm)] + [0, regions + 1]:
        pltpu.make_async_copy(t_in.at[slot], t_in.at[slot], t_recv.at[slot]).wait()
        place(slot, t_in[slot])

    for copy in edge_copies + inner_copies + t_copies:
        copy.wait_send()

    @pl.when(tm == 0)
    def _():
        for copy in low:
            copy.wait_send()

    @pl.when(tm == n_tm - 1)
    def _():
        for copy in high:
            copy.wait_send()


def analyse(transform_ref, states_ref, out_ref):
    region = pl.program_id(1)
    x = states_ref[0, 0].astype(F32)
    rows, members = x.shape
    mean = jnp.sum(x, axis=1, keepdims=True) * (1.0 / members)
    anomaly = (x - mean).astype(BF16)
    mid = rows // 2

    def apply(block, slot):
        return lax.dot_general(
            block, transform_ref[slot], (((1,), (1,)), ((), ())), preferred_element_type=F32
        )

    centre = apply(anomaly, region + 1)
    beside = jnp.concatenate(
        [apply(anomaly[:mid], region), apply(anomaly[mid:], region + 2)], axis=0
    )
    column = iota2((rows, 1), 0) // (rows // HC)
    blend = jnp.abs((column.astype(F32) + 0.5) / HC - 0.5)
    out_ref[0, 0] = (mean + centre + blend * (beside - centre)).astype(BF16)


def shards(n_tm, n_space, obs, innovation, error_weight, obs_column, obs_count, radius, states):
    _, regions, capacity, members = obs.shape
    assert regions == n_tm and obs.shape[0] == 1
    rows = members // 2 + EXTRA
    vmem = pl.BlockSpec(memory_space=pltpu.VMEM)
    smem = pl.BlockSpec(memory_space=pltpu.SMEM)
    hbm = pl.BlockSpec(memory_space=pl.ANY)
    dma = pltpu.SemaphoreType.DMA
    transforms = pl.pallas_call(
        functools.partial(assimilate, n_tm, n_space),
        out_shape=jax.ShapeDtypeStruct((regions + 2, members, members), BF16),
        in_specs=[smem, smem, hbm, vmem, vmem, vmem],
        out_specs=vmem,
        scratch_shapes=[
            pltpu.VMEM((regions, capacity, members), BF16),
            pltpu.VMEM((regions, members, capacity), BF16),
            pltpu.VMEM((regions + 2 * HALO, rows, members), BF16),
            pltpu.VMEM((2, n_tm, rows, members), BF16),
            pltpu.VMEM((rows, members), BF16),
            pltpu.VMEM((rows, members), BF16),
            pltpu.VMEM((rows, members), BF16),
            pltpu.VMEM((regions + 2, rows, members), BF16),
            dma((regions,)),
            dma((2, n_tm - 1)),
            dma((2, n_tm)),
            dma,
            dma,
            dma((n_tm - 1,)),
            dma((n_tm,)),
            dma((regions + 2,)),
        ],
        compiler_params=pltpu.CompilerParams(
            collective_id=0, has_side_effects=True, vmem_limit_bytes=40 * 2**20
        ),
        name="assimilate",
    )(obs_count, radius, obs, innovation, error_weight, obs_column)
    lags, columns, levels, _ = states.shape
    shaped = states.reshape(lags, regions, columns // regions * levels, members)
    block = pl.BlockSpec((1, 1) + shaped.shape[2:], lambda i, j: (i, j, 0, 0))
    result = pl.pallas_call(
        analyse,
        grid=(lags, regions),
        out_shape=jax.ShapeDtypeStruct(shaped.shape, BF16),
        in_specs=[vmem, block],
        out_specs=block,
        compiler_params=pltpu.CompilerParams(vmem_limit_bytes=20 * 2**20),
        name="analyse",
    )(transforms, shaped)
    return result.reshape(states.shape)


def solution(mesh):
    return jax.shard_map(
        functools.partial(shards, mesh.shape["tm"], mesh.shape["space"]),
        mesh=mesh,
        in_specs=(
            P("tm", "space", None, None),
            P("tm", "space", None),
            P("tm", "space", None),
            P("tm", "space", None),
            P("tm", "space"),
            P("space"),
            P("tm", "space", None, None),
        ),
        out_specs=P("tm", "space", None, None),
        check_vma=False,
    )
```

time: 103 us -> 36.5 us (0.35); the launches traced: 101 us -> 36.1 us
  Pallas kernels: 0 us -> 31 us
  matrix products: 30.5 us -> 0 us
  blocking collectives: 14.9 us -> 0 us
  between operations: 14.5 us -> 0.02 us
  waiting for transfers between devices: 14.2 us -> 0 us
  starting transfers between devices: 13.7 us -> 0 us
  other arithmetic: 7.28 us -> 0 us
    pallas_call x0 -> x2, Pallas kernels: none -> 31 us  [the longest x1 26.2 us: shards(): pl.pallas_call(functools.partial(assimilate, n_tm, n_space), out_shape=ja...]
    dot_general x29 -> x0, matrix products: 30.5 us -> none  [the longest x5 11 us: shards(): jnp.einsum('srok,srol->rkl', weighted, obs_perturb, preferred_element_typ...]
    ppermute x6 -> x0, starting transfers between devices: 13.7 us -> none  [the longest x3 10 us: with_halo(): lax.ppermute(lax.slice_in_dim(block, 0, width, axis=dim), axis, backward)]
    unnamed x1 -> x0, blocking collectives: 7.67 us -> none
    all_gather x1 -> x0, blocking collectives: 7.28 us -> none  [shards(): transform = lax.all_gather(local_transform, 'tm', axis=0, tiled=True)]
    reduce_scatter x1 -> x0, waiting for transfers between devices: 7.12 us -> none  [shards(): lax.psum_scatter(inner_gram, 'tm', scatter_dimension=0, tiled=True)]
    ppermute x6 -> x0, waiting for transfers between devices: 7.03 us -> none  [the longest x3 3.87 us: with_halo(): lax.ppermute(lax.slice_in_dim(block, 0, width, axis=dim), axis, backward)]
    unnamed x13 -> x14, local copies, waits for them, and re-layouts: 0.65 us -> 5.05 us
  transfers between devices with their start and end apart: 7 -> 0, of which waited for: 4 -> 0; matrix products, arithmetic and copies ran while one was open for 16% -> 0% of each run, Pallas kernels for 0% -> 0%
where the time goes in v1:
time: 36.5 us; the launch traced here: 36.1 us
  Pallas kernels  31 us (85%)
  local copies, waits for them, and re-layouts  5.05 us (14%)
    pallas_call x1, Pallas kernels, shards(): pl.pallas_call(functools.partial(assimilate, n_tm, n_space), out_shape=ja...  26.2 us
    unnamed x14, local copies, waits for them, and re-layouts  5.05 us
    pallas_call x1, Pallas kernels, shards(): pl.pallas_call(analyse, grid=(lags, regions), out_shape=jax.ShapeDtypeStr...  4.79 us

profile of v1, /device:TPU:1, one launch (start us, length us, event | category | flops | bytes accessed | tf_op | source)
XLA Modules:
  0.0 36.1 jit_solution(10914546442700032392)
XLA Ops:
  0.0 0.0 copy-start
  0.0 1.6 %copy-done = bf16[1,4,1024,256]{3,2,1,0:T(8,128)(2,1)S(1)} copy-done((bf16[1,4,1024,256]{3,2,1,0:T(8,128)(2,1)S(1)}, bf16[1,4,1024,256]{3,2,1,0:T(8,128)(2,1)}, u32[]{:S(2)}) %copy-start) | copy-done | bytes 2097176
  1.6 0.0 copy-start.2
  1.6 0.7 %copy-done.2 = f32[1,4,1024]{2,1,0:T(4,128)S(1)} copy-done((f32[1,4,1024]{2,1,0:T(4,128)S(1)}, f32[1,4,1024]{2,1,0:T(4,128)}, u32[]{:S(2)}) %copy-start.2) | copy-done | bytes 16408
  2.3 0.0 copy-start.3
  2.3 0.7 %copy-done.3 = f32[1,4,1024]{2,1,0:T(4,128)S(1)} copy-done((f32[1,4,1024]{2,1,0:T(4,128)S(1)}, f32[1,4,1024]{2,1,0:T(4,128)}, u32[]{:S(2)}) %copy-start.3) | copy-done | bytes 16408
  3.0 0.0 copy-start.4
  3.0 0.7 %copy-done.4 = s32[1,4,1024]{2,1,0:T(4,128)S(1)} copy-done((s32[1,4,1024]{2,1,0:T(4,128)S(1)}, s32[1,4,1024]{2,1,0:T(4,128)}, u32[]{:S(2)}) %copy-start.4) | copy-done | bytes 16408
  3.7 0.0 copy-start.5
  3.7 0.7 %copy-done.5 = s32[1,4]{1,0:T(1,128)S(1)} copy-done((s32[1,4]{1,0:T(1,128)S(1)}, s32[1,4]{1,0:T(1,128)}, u32[]{:S(2)}) %copy-start.5) | copy-done | bytes 40
  4.4 0.0 copy-start.6
  4.4 0.7 %copy-done.6 = s32[4]{0:T(128)S(1)} copy-done((s32[4]{0:T(128)S(1)}, s32[4]{0:T(128)}, u32[]{:S(2)}) %copy-start.6) | copy-done | bytes 40
  5.1 0.0 copy-start.1
  5.1 26.2 %assimilate.1.transform_ref = bf16[6,256,256]{2,1,0:T(8,128)(2,1)S(1)} custom-call(s32[1,4]{1,0:T(1,128)S(1)} %copy-done.5, s32[4]{0:T(128)S(1)} %copy-done.6, bf16[1,4,1024,256]{3,2,1,0:T(8,128)(2,1)S(1)} %copy-done, f32[1,4,1024]{2,1,0:T(4,128)S(1)} %copy-done.2, f32[1,4,1024]{2,1,0:T(4,128)S(1)} %copy-done.3, s32[1,4,1024]{2,1,0:T(4,128)S(1)} %copy-done.4), custom_call_target="tpu_custom_call" | custom-call | tf_op jit(solution)/shard_map/assimilate/pallas_call | solution.py:292
  31.3 0.0 copy-done.1
  31.3 4.8 %analyse.1 = bf16[2,4,512,256]{3,2,1,0:T(8,128)(2,1)} custom-call(bf16[6,256,256]{2,1,0:T(8,128)(2,1)S(1)} %assimilate.1.transform_ref, bf16[2,4,512,256]{3,2,1,0:T(8,128)(2,1)S(1)} %bitcast.2), custom_call_target="tpu_custom_call" | custom-call | tf_op jit(solution)/shard_map/analyse/pallas_call | solution.py:323
Async XLA Ops:
  0.0 1.6 %copy-start = (bf16[1,4,1024,256]{3,2,1,0:T(8,128)(2,1)S(1)}, bf16[1,4,1024,256]{3,2,1,0:T(8,128)(2,1)}, u32[]{:S(2)}) copy-start(bf16[1,4,1024,256]{3,2,1,0:T(8,128)(2,1)} %obs_hbm.1) | copy-start | bytes 6291460
  1.6 0.7 %copy-start.2 = (f32[1,4,1024]{2,1,0:T(4,128)S(1)}, f32[1,4,1024]{2,1,0:T(4,128)}, u32[]{:S(2)}) copy-start(f32[1,4,1024]{2,1,0:T(4,128)} %innov_ref.1) | copy-start | bytes 49156
  2.3 0.7 %copy-start.3 = (f32[1,4,1024]{2,1,0:T(4,128)S(1)}, f32[1,4,1024]{2,1,0:T(4,128)}, u32[]{:S(2)}) copy-start(f32[1,4,1024]{2,1,0:T(4,128)} %weight_ref.1) | copy-start | bytes 49156
  3.0 0.7 %copy-start.4 = (s32[1,4,1024]{2,1,0:T(4,128)S(1)}, s32[1,4,1024]{2,1,0:T(4,128)}, u32[]{:S(2)}) copy-start(s32[1,4,1024]{2,1,0:T(4,128)} %column_ref.1) | copy-start | bytes 49156
  3.7 0.7 %copy-start.5 = (s32[1,4]{1,0:T(1,128)S(1)}, s32[1,4]{1,0:T(1,128)}, u32[]{:S(2)}) copy-start(s32[1,4]{1,0:T(1,128)} %count_ref.1) | copy-start | bytes 52
  4.4 0.7 %copy-start.6 = (s32[4]{0:T(128)S(1)}, s32[4]{0:T(128)}, u32[]{:S(2)}) copy-start(s32[4]{0:T(128)} %radius_ref.1) | copy-start | bytes 52
  5.1 26.2 %copy-start.1 = (bf16[2,128,16,256]{3,2,1,0:T(8,128)(2,1)S(1)}, bf16[2,128,16,256]{3,2,1,0:T(8,128)(2,1)}, u32[]{:S(2)}) copy-start(bf16[2,128,16,256]{3,2,1,0:T(8,128)(2,1)} %param.13) | copy-start | bytes 6291460

commit v2 on v1

--- a/solution.py
+++ b/solution.py
@@ -90,9 +90,9 @@
 
 def assimilate(
     n_tm, n_space,
-    count_ref, radius_ref, obs_hbm, innov_ref, weight_ref, column_ref, out_ref,
-    obs_v, obs_t, mine, recv, halo_out, halo_in, t_out, t_in,
-    load_sem, rs_send, rs_recv, halo_send, halo_recv, t_send, b_send, t_recv,
+    count_hbm, radius_hbm, obs_hbm, innov_hbm, weight_hbm, column_hbm, states_hbm, out_ref,
+    count_ref, radius_ref, innov_ref, weight_ref, column_ref, anomaly, means, tmat, obs_v, obs_t, mine, recv, halo_out, halo_in, t_out, t_in,
+    load_sem, small_sem, rs_send, rs_recv, halo_send, halo_recv, t_send, b_send, t_recv,
 ):
     tm, sp = lax.axis_index("tm"), lax.axis_index("space")
     after, before = lax.rem(sp + 1, n_space), lax.rem(sp + n_space - 1, n_space)
@@ -103,7 +103,20 @@
     loads = [
         pltpu.make_async_copy(obs_hbm.at[0, r], obs_v.at[r], load_sem.at[r]) for r in range(regions)
     ]
-    for load in loads:
+    small = [
+        pltpu.make_async_copy(src, dst, small_sem.at[n])
+        for n, (src, dst) in enumerate(
+            [
+                (count_hbm, count_ref),
+                (radius_hbm, radius_ref),
+                (innov_hbm.at[0], innov_ref),
+                (weight_hbm.at[0], weight_ref),
+                (column_hbm.at[0], column_ref),
+                (states_hbm, anomaly),
+            ]
+        )
+    ]
+    for load in small[:-1] + loads + small[-1:]:
         load.start()
 
     barrier = pltpu.get_barrier_semaphore()
@@ -112,6 +125,12 @@
     greeted += [(t, s) for s in (before, after) for t in range(n_tm)]
     for t, s in greeted:
         pl.semaphore_signal(barrier, inc=1, device_id={"tm": t, "space": s}, device_id_type=MESH)
+
+    for r in range(regions):
+        loads[r].wait()
+        obs_t[r] = obs_v[r].T
+    for load in small[:-1]:
+        load.wait()
 
     shape = (regions, capacity)
     which = iota2(shape, 0)
@@ -121,15 +140,15 @@
         count = jnp.where(which == r, count_ref[0, r], count)
         radius = jnp.where(which == r, radius_ref[r], radius)
     present = (iota2(shape, 1) < count).astype(F32)
-    base = weight_ref[0] * present
+    base = weight_ref[...] * present
     inverse_radius = 1.0 / radius.astype(F32)
-    position = column_ref[0].astype(F32) + 0.5 - 0.5 * HC
+    position = column_ref[...].astype(F32) + 0.5 - 0.5 * HC
     weights, pulls = [], []
     for offset in range(-HALO, HALO + 1):
         ratio = jnp.minimum(jnp.abs(position - offset * HC) * inverse_radius, 1.0)
         weight = base * jnp.square(1.0 - ratio * ratio)
         weights.append(weight)
-        pulls.append(weight * innov_ref[0])
+        pulls.append(weight * innov_ref[...])
 
     first_row = iota2((EXTRA, capacity), 0) == 0
 
@@ -171,14 +190,10 @@
             total = total + recv[kind, peer].astype(F32)
         return total
 
-    for r in range(regions):
-        loads[r].wait()
-        obs_t[r] = obs_v[r].T
-    pl_wait = len(greeted)
     edges = [*range(HALO), *range(targets - HALO, targets)]
     for target in edges:
         gram_of(target)
-    pl.semaphore_wait(barrier, pl_wait)
+    pl.semaphore_wait(barrier, len(greeted))
     edge_block = lambda p: lax.rem(p + regions + HALO, targets)
     inner_block = lambda p: p + HALO
     edge_copies = exchange(0, edge_block)
@@ -190,6 +205,19 @@
     inner_copies = exchange(1, inner_block)
     for copy in inner_copies:
         copy.start()
+
+    small[-1].wait()
+    lags, _, rows, _ = anomaly.shape
+
+    def centre_on_mean(n, carry):
+        lag, r = n // regions, lax.rem(n, regions)
+        x = anomaly[lag, r].astype(F32)
+        mean = jnp.sum(x, axis=1, keepdims=True) * (1.0 / members)
+        means[lag, r] = mean
+        anomaly[lag, r] = (x - mean).astype(BF16)
+        return carry
+
+    lax.fori_loop(0, lags * regions, centre_on_mean, 0)
 
     halo_out[...] = collect(0, edge_block(tm)).astype(BF16)
     halo_copy = pltpu.make_async_remote_copy(
@@ -238,12 +266,41 @@
 
     def place(slot, block):
         matrix, row = unpack(block.astype(F32))
-        out_ref[slot] = (matrix + row).astype(BF16)
-
-    place(tm + 1, t_out[...])
-    for slot in [lax.rem(tm + d, n_tm) + 1 for d in range(1, n_tm)] + [0, regions + 1]:
+        tmat[slot] = (matrix + row).astype(BF16)
+
+    def arrive(slot):
         pltpu.make_async_copy(t_in.at[slot], t_in.at[slot], t_recv.at[slot]).wait()
         place(slot, t_in[slot])
+
+    mid = rows // 2
+
+    def update(r, side):
+        part = slice(side * mid, (side + 1) * mid)
+        column = (iota2((mid, 1), 0) + side * mid) // (rows // HC)
+        blend = jnp.abs((column.astype(F32) + 0.5) / HC - 0.5)
+        for lag in range(lags):
+            block = anomaly[lag, r, part]
+
+            def apply(slot):
+                return lax.dot_general(
+                    block, tmat[slot], (((1,), (1,)), ((), ())), preferred_element_type=F32
+                )
+
+            centre, beside = apply(r + 1), apply(r + 2 * side)
+            mean = means[lag, r, part]
+            out_ref[lag, r, part] = (mean + centre + blend * (beside - centre)).astype(BF16)
+
+    place(tm + 1, t_out[...])
+    for d in range(1, n_tm):
+        arrive(lax.rem(tm + d, n_tm) + 1)
+    for r in range(regions):
+        for side in range(2):
+            if (r, side) not in ((0, 0), (regions - 1, 1)):
+                update(r, side)
+    arrive(0)
+    update(0, 0)
+    arrive(regions + 1)
+    update(regions - 1, 1)
 
     for copy in edge_copies + inner_copies + t_copies:
         copy.wait_send()
@@ -259,42 +316,28 @@
             copy.wait_send()
 
 
-def analyse(transform_ref, states_ref, out_ref):
-    region = pl.program_id(1)
-    x = states_ref[0, 0].astype(F32)
-    rows, members = x.shape
-    mean = jnp.sum(x, axis=1, keepdims=True) * (1.0 / members)
-    anomaly = (x - mean).astype(BF16)
-    mid = rows // 2
-
-    def apply(block, slot):
-        return lax.dot_general(
-            block, transform_ref[slot], (((1,), (1,)), ((), ())), preferred_element_type=F32
-        )
-
-    centre = apply(anomaly, region + 1)
-    beside = jnp.concatenate(
-        [apply(anomaly[:mid], region), apply(anomaly[mid:], region + 2)], axis=0
-    )
-    column = iota2((rows, 1), 0) // (rows // HC)
-    blend = jnp.abs((column.astype(F32) + 0.5) / HC - 0.5)
-    out_ref[0, 0] = (mean + centre + blend * (beside - centre)).astype(BF16)
-
-
 def shards(n_tm, n_space, obs, innovation, error_weight, obs_column, obs_count, radius, states):
     _, regions, capacity, members = obs.shape
     assert regions == n_tm and obs.shape[0] == 1
     rows = members // 2 + EXTRA
-    vmem = pl.BlockSpec(memory_space=pltpu.VMEM)
-    smem = pl.BlockSpec(memory_space=pltpu.SMEM)
-    hbm = pl.BlockSpec(memory_space=pl.ANY)
+    lags, columns, levels, _ = states.shape
+    shaped = states.reshape(lags, regions, columns // regions * levels, members)
+    hbm = pl.BlockSpec(memory_space=pltpu.HBM)
     dma = pltpu.SemaphoreType.DMA
-    transforms = pl.pallas_call(
+    result = pl.pallas_call(
         functools.partial(assimilate, n_tm, n_space),
-        out_shape=jax.ShapeDtypeStruct((regions + 2, members, members), BF16),
-        in_specs=[smem, smem, hbm, vmem, vmem, vmem],
-        out_specs=vmem,
+        out_shape=pltpu.VMEM(shaped.shape, BF16),
+        in_specs=[hbm] * 7,
+        out_specs=pl.BlockSpec(memory_space=pltpu.VMEM),
         scratch_shapes=[
+            pltpu.SMEM(obs_count.shape, jnp.int32),
+            pltpu.SMEM(radius.shape, jnp.int32),
+            pltpu.VMEM((regions, capacity), F32),
+            pltpu.VMEM((regions, capacity), F32),
+            pltpu.VMEM((regions, capacity), jnp.int32),
+            pltpu.VMEM(shaped.shape, BF16),
+            pltpu.VMEM(shaped.shape[:-1] + (1,), F32),
+            pltpu.VMEM((regions + 2, members, members), BF16),
             pltpu.VMEM((regions, capacity, members), BF16),
             pltpu.VMEM((regions, members, capacity), BF16),
             pltpu.VMEM((regions + 2 * HALO, rows, members), BF16),
@@ -304,6 +347,7 @@
             pltpu.VMEM((rows, members), BF16),
             pltpu.VMEM((regions + 2, rows, members), BF16),
             dma((regions,)),
+            dma((6,)),
             dma((2, n_tm - 1)),
             dma((2, n_tm)),
             dma,
@@ -313,22 +357,10 @@
             dma((regions + 2,)),
         ],
         compiler_params=pltpu.CompilerParams(
-            collective_id=0, has_side_effects=True, vmem_limit_bytes=40 * 2**20
+            collective_id=0, has_side_effects=True, vmem_limit_bytes=67043328 - 2228224
         ),
         name="assimilate",
-    )(obs_count, radius, obs, innovation, error_weight, obs_column)
-    lags, columns, levels, _ = states.shape
-    shaped = states.reshape(lags, regions, columns // regions * levels, members)
-    block = pl.BlockSpec((1, 1) + shaped.shape[2:], lambda i, j: (i, j, 0, 0))
-    result = pl.pallas_call(
-        analyse,
-        grid=(lags, regions),
-        out_shape=jax.ShapeDtypeStruct(shaped.shape, BF16),
-        in_specs=[vmem, block],
-        out_specs=block,
-        compiler_params=pltpu.CompilerParams(vmem_limit_bytes=20 * 2**20),
-        name="analyse",
-    )(transforms, shaped)
+    )(obs_count, radius, obs, innovation, error_weight, obs_column, shaped)
     return result.reshape(states.shape)
 
 

time: 36.5 us -> 28.5 us (0.78)
  Pallas kernels: 31 us -> 27.1 us
  local copies, waits for them, and re-layouts: 5.05 us -> 1.32 us
    pallas_call x2 -> x1, Pallas kernels: 31 us -> 27.1 us  [shards(): pl.pallas_call(functools.partial(assimilate, n_tm, n_space), out_shape=pl...]
    unnamed x14 -> x1, local copies, waits for them, and re-layouts: 5.05 us -> 1.32 us
where the time goes in v2:
time: 28.5 us; the launch traced here: 28.4 us
  Pallas kernels  27.1 us (95%)
  local copies, waits for them, and re-layouts  1.32 us (5%)
    pallas_call x1, Pallas kernels, shards(): pl.pallas_call(functools.partial(assimilate, n_tm, n_space), out_shape=pl...  27.1 us
    unnamed x1, local copies, waits for them, and re-layouts  1.32 us

profile of v2, /device:TPU:1, one launch (start us, length us, event | category | flops | bytes accessed | tf_op | source)
XLA Modules:
  0.0 28.4 jit_solution(9074003531366579849)
XLA Ops:
  0.0 27.1 %assimilate.1 = bf16[2,4,512,256]{3,2,1,0:T(8,128)(2,1)S(1)} custom-call(s32[1,4]{1,0:T(1,128)} %count_hbm.1, s32[4]{0:T(128)} %radius_hbm.1, bf16[1,4,1024,256]{3,2,1,0:T(8,128)(2,1)} %obs_hbm.1, f32[1,4,1024]{2,1,0:T(4,128)} %innov_hbm.1, f32[1,4,1024]{2,1,0:T(4,128)} %weight_hbm.1, s32[1,4,1024]{2,1,0:T(4,128)} %column_hbm.1, bf16[2,4,512,256]{3,2,1,0:T(8,128)(2,1)} %bitcast.3), custom_call_target="tpu_custom_call" | custom-call | tf_op jit(solution)/shard_map/assimilate/pallas_call | solution.py:327
  27.1 1.3 %copy.9 = bf16[2,128,16,256]{3,2,1,0:T(8,128)(2,1)} copy(bf16[2,128,16,256]{3,2,1,0:T(8,128)(2,1)S(1)} %bitcast.2) | data formatting | bytes 4194304

commit v3 on v2

--- a/solution.py
+++ b/solution.py
@@ -126,9 +126,6 @@
     for t, s in greeted:
         pl.semaphore_signal(barrier, inc=1, device_id={"tm": t, "space": s}, device_id_type=MESH)
 
-    for r in range(regions):
-        loads[r].wait()
-        obs_t[r] = obs_v[r].T
     for load in small[:-1]:
         load.wait()
 
@@ -166,43 +163,53 @@
         mine[target, :half] = top.astype(BF16)
         mine[target, half:] = extra.astype(BF16)
 
-    def exchange(kind, block_of):
+    height = mine.shape[1]
+    whole = pl.ds(0, height)
+    cut = height // (2 * EXTRA) * EXTRA
+    chunks = [pl.ds(0, cut), pl.ds(cut, height - cut)]
+
+    def exchange(kind, sem, block_of, rows):
         copies = []
         for d, peer in enumerate(peers):
             copies.append(
                 pltpu.make_async_remote_copy(
-                    src_ref=mine.at[block_of(peer)],
-                    dst_ref=recv.at[kind, tm],
-                    send_sem=rs_send.at[kind, d],
-                    recv_sem=rs_recv.at[kind, tm],
+                    src_ref=mine.at[block_of(peer), rows],
+                    dst_ref=recv.at[kind, tm, rows],
+                    send_sem=rs_send.at[sem, d],
+                    recv_sem=rs_recv.at[sem, tm],
                     device_id={"tm": peer, "space": sp},
                     device_id_type=MESH,
                 )
             )
         return copies
 
-    def collect(kind, block):
-        total = mine[block].astype(F32)
+    def collect(kind, sem, block, rows):
+        total = mine[block, rows].astype(F32)
         for peer in peers:
-            pltpu.make_async_copy(
-                recv.at[kind, peer], recv.at[kind, peer], rs_recv.at[kind, peer]
-            ).wait()
-            total = total + recv[kind, peer].astype(F32)
+            landed = recv.at[kind, peer, rows]
+            pltpu.make_async_copy(landed, landed, rs_recv.at[sem, peer]).wait()
+            total = total + recv[kind, peer, rows].astype(F32)
         return total
 
-    edges = [*range(HALO), *range(targets - HALO, targets)]
-    for target in edges:
+    ready = 0
+    for target in [*range(HALO), *range(targets - HALO, targets)]:
+        while ready < min(regions, target + 1):
+            loads[ready].wait()
+            obs_t[ready] = obs_v[ready].T
+            ready += 1
         gram_of(target)
     pl.semaphore_wait(barrier, len(greeted))
     edge_block = lambda p: lax.rem(p + regions + HALO, targets)
     inner_block = lambda p: p + HALO
-    edge_copies = exchange(0, edge_block)
+    edge_copies = []
+    for c, part in enumerate(chunks):
+        edge_copies += exchange(0, c + 1, edge_block, part)
     for copy in edge_copies:
         copy.start()
     inner = list(range(HALO, targets - HALO))
     for target in inner:
         gram_of(target)
-    inner_copies = exchange(1, inner_block)
+    inner_copies = exchange(1, 0, inner_block, whole)
     for copy in inner_copies:
         copy.start()
 
@@ -219,18 +226,23 @@
 
     lax.fori_loop(0, lags * regions, centre_on_mean, 0)
 
-    halo_out[...] = collect(0, edge_block(tm)).astype(BF16)
-    halo_copy = pltpu.make_async_remote_copy(
-        src_ref=halo_out,
-        dst_ref=halo_in,
-        send_sem=halo_send,
-        recv_sem=halo_recv,
-        device_id={"tm": tm, "space": jnp.where(tm < HALO, after, before)},
-        device_id_type=MESH,
-    )
-    halo_copy.start()
-    total = collect(1, inner_block(tm))
-    halo_copy.wait()
+    halo_copies = []
+    for c, part in enumerate(chunks):
+        halo_out[part] = collect(0, c + 1, edge_block(tm), part).astype(BF16)
+        halo_copies.append(
+            pltpu.make_async_remote_copy(
+                src_ref=halo_out.at[part],
+                dst_ref=halo_in.at[part],
+                send_sem=halo_send.at[c],
+                recv_sem=halo_recv.at[c],
+                device_id={"tm": tm, "space": jnp.where(tm < HALO, after, before)},
+                device_id_type=MESH,
+            )
+        )
+        halo_copies[c].start()
+    total = collect(1, 0, inner_block(tm), whole)
+    for copy in halo_copies:
+        copy.wait()
     gram, vec = unpack(total + halo_in[...].astype(F32))
     spread, wbar = transform_parts(gram, vec)
     top, extra = pack(spread, wbar)
@@ -252,7 +264,7 @@
 
     @pl.when(tm == 0)
     def _():
-        for copy in low:
+        for copy in reversed(low):
             copy.start()
 
     @pl.when(tm == n_tm - 1)
@@ -348,10 +360,10 @@
             pltpu.VMEM((regions + 2, rows, members), BF16),
             dma((regions,)),
             dma((6,)),
-            dma((2, n_tm - 1)),
-            dma((2, n_tm)),
-            dma,
-            dma,
+            dma((3, n_tm - 1)),
+            dma((3, n_tm)),
+            dma((2,)),
+            dma((2,)),
             dma((n_tm - 1,)),
             dma((n_tm,)),
             dma((regions + 2,)),

time: 28.5 us -> 28.6 us (level)
  no operation moved by 1% of the time
where the time goes in v3:
time: 28.6 us; the launch traced here: 28.5 us
  Pallas kernels  27.1 us (95%)
  local copies, waits for them, and re-layouts  1.32 us (5%)
    pallas_call x1, Pallas kernels, shards(): pl.pallas_call(functools.partial(assimilate, n_tm, n_space), out_shape=pl...  27.1 us
    unnamed x1, local copies, waits for them, and re-layouts  1.32 us

profile of v3, /device:TPU:1, one launch (start us, length us, event | category | flops | bytes accessed | tf_op | source)
XLA Modules:
  0.0 28.5 jit_solution(5830288134792650111)
XLA Ops:
  0.0 27.1 %assimilate.1 = bf16[2,4,512,256]{3,2,1,0:T(8,128)(2,1)S(1)} custom-call(s32[1,4]{1,0:T(1,128)} %count_hbm.1, s32[4]{0:T(128)} %radius_hbm.1, bf16[1,4,1024,256]{3,2,1,0:T(8,128)(2,1)} %obs_hbm.1, f32[1,4,1024]{2,1,0:T(4,128)} %innov_hbm.1, f32[1,4,1024]{2,1,0:T(4,128)} %weight_hbm.1, s32[1,4,1024]{2,1,0:T(4,128)} %column_hbm.1, bf16[2,4,512,256]{3,2,1,0:T(8,128)(2,1)} %bitcast.3), custom_call_target="tpu_custom_call" | custom-call | tf_op jit(solution)/shard_map/assimilate/pallas_call | solution.py:339
  27.1 1.3 %copy.9 = bf16[2,128,16,256]{3,2,1,0:T(8,128)(2,1)} copy(bf16[2,128,16,256]{3,2,1,0:T(8,128)(2,1)S(1)} %bitcast.2) | data formatting | bytes 4194304
